TPU v7x, 32 devices: a whole 2x2x4 slice. The times are simulated.
32 devices in a mesh: parts: 2 (over y), expert: 4 (over z), tensor: 4 (over x, core).
Axes of the slice: x: 2, y: 2, z: 4, core: 2. Of those that a mesh axis runs over, the one named last changes fastest.
Arguments:
- tokens: bfloat16 [128, 6144], P(('parts', 'expert'), 'tensor'), parts along dimension 0, may hold values from -4 to 4
- queries: bfloat16 [128, 48, 128], P(('parts', 'expert'), 'tensor'), parts along dimension 0, may hold values from -6 to 6
- new_kv: bfloat16 [2, 128, 8, 128], P(None, ('parts', 'expert'), 'tensor'), parts along dimension 1, may hold values from -6 to 6
- cache_kv: bfloat16 [2, 128, 16, 8, 128], P(None, ('parts', 'expert'), None, 'tensor'), parts along dimension 1, may hold values from -6 to 6
- lengths: int32 [128], P(('parts', 'expert')), parts along dimension 0, may hold values from 2 to 16
- gain: float32 [6144], P('tensor'), may hold values from 0.1 to 1.9
- gate_weight: bfloat16 [6144, 32768], P('tensor', 'expert'), may hold values from -0.078125 to 0.078125
- up_weight: bfloat16 [6144, 32768], P('tensor', 'expert'), may hold values from -0.078125 to 0.078125
- down_weight: bfloat16 [32768, 6144], P('expert', 'tensor'), may hold values from -0.0625 to 0.0625
- routes: int32 [128, 2], P(('parts', 'expert')), parts along dimension 0, may hold values from 0 to 3, all different within a row; in each aligned block of 16 rows (0 to 15, 16 to 31, ...) at most 9 rows name the same one
- route_weights: bfloat16 [128, 2], P(('parts', 'expert')), parts along dimension 0, may hold values from 0.19921875 to 0.796875
Outputs:
- mixed: bfloat16 [128, 6144], P(('parts', 'expert'), 'tensor'), parts along dimension 0
There are 2 independent parts, one for each index of `parts`. A program takes and returns all parts, laid end to end along the dimension named above; an argument that names none is the same for every part. Nothing has to cross between parts.
Inputs may be any that keep to these rules, and one draw needn't show every extreme that they name: `routes`: the two entries of a row differ; in the rows of one index of expert no expert is named more than 9 times, a bound that some block reaches there in every draw.
All inputs are finite; a program needn't handle non-finite values.
Results may differ from a plain program's by a relative error of at most 0.0094.
Values may be sent and summed in bfloat16 or wider, within the bound.
A program may use at most 128 MiB of HBM per device.

v0:
```python
import functools
import math

import jax
import jax.numpy as jnp
from jax import lax
from jax.experimental import pallas as pl
from jax.experimental.pallas import tpu as pltpu
from jax.sharding import PartitionSpec as P

EXPERTS = 4
CAP = 9


EPSILON = 1e-05


def attend(queries, new_kv, cache_kv, lengths):
    sequences, head_count, head_size = queries.shape
    key_heads = new_kv.shape[2]
    groups = head_count // key_heads
    factor = 1.0 / math.sqrt(head_size)
    query_grp = queries.reshape(sequences, key_heads, groups, head_size)
    score_old = (
        jnp.einsum("skgd,spkd->skgp", query_grp, cache_kv[0], preferred_element_type=jnp.float32)
        * factor
    )
    score_new = (
        jnp.einsum("skgd,skd->skg", query_grp, new_kv[0], preferred_element_type=jnp.float32)
        * factor
    )
    position = jnp.arange(cache_kv.shape[2], dtype=jnp.int32)
    usable = (position[None, :] < lengths[:, None])[:, None, None, :]
    score_old = jnp.where(usable, score_old, -jnp.inf)
    largest = jnp.maximum(jnp.max(score_old, axis=3), score_new)
    weight_old = jnp.exp(score_old - largest[..., None])
    weight_new = jnp.exp(score_new - largest)
    denominator = jnp.sum(weight_old, axis=3) + weight_new
    prob_old = (weight_old / denominator[..., None]).astype(jnp.bfloat16)
    prob_new = (weight_new / denominator).astype(jnp.bfloat16)
    attended = jnp.einsum(
        "skgp,spkd->skgd", prob_old, cache_kv[1], preferred_element_type=jnp.float32
    )
    attended = (
        attended
        + prob_new.astype(jnp.float32)[..., None] * new_kv[1].astype(jnp.float32)[:, :, None, :]
    )
    return attended.reshape(sequences, head_count * head_size)


def expert_hidden(token_rows, gate_weight, up_weight, down_weight):
    gate_sum = jnp.dot(token_rows, gate_weight, preferred_element_type=jnp.float32)
    lift_sum = jnp.dot(token_rows, up_weight, preferred_element_type=jnp.float32)
    gate_sum, lift_sum = (
        lax.psum_scatter(gate_sum, "tensor", scatter_dimension=1, tiled=True),
        lax.psum_scatter(lift_sum, "tensor", scatter_dimension=1, tiled=True),
    )
    hidden = (jax.nn.silu(gate_sum) * lift_sum).astype(jnp.bfloat16)
    hidden = lax.all_gather(hidden, "tensor", axis=1, tiled=True)
    return jnp.dot(hidden, down_weight, preferred_element_type=jnp.float32)


def pack_slots(target, normed):
    slot_ids = jnp.arange(EXPERTS * CAP, dtype=jnp.int32)
    placing = (slot_ids[:, None, None] == target[None, :, :]).astype(jnp.float32)
    placing = jnp.sum(placing, axis=2).astype(jnp.bfloat16)
    packed = jnp.dot(placing, normed, preferred_element_type=jnp.float32).astype(jnp.bfloat16)
    return packed.reshape(EXPERTS, CAP, normed.shape[1])


def mix_slots(target, route_weights, per_slot):
    slot_ids = jnp.arange(EXPERTS * CAP, dtype=jnp.int32)
    mixing = jnp.where(
        slot_ids[None, None, :] == target[:, :, None],
        route_weights.astype(jnp.float32)[:, :, None],
        jnp.float32(0.0),
    )
    mixing = jnp.sum(mixing, axis=1)
    return jnp.dot(
        mixing, per_slot, precision=lax.Precision.HIGHEST, preferred_element_type=jnp.float32
    )


def on_device(
    tokens,
    queries,
    new_kv,
    cache_kv,
    lengths,
    gain,
    gate_weight,
    up_weight,
    down_weight,
    routes,
    route_weights,
):
    local_seqs, local_width = tokens.shape
    residual = tokens.astype(jnp.float32) + attend(queries, new_kv, cache_kv, lengths)
    full_width = local_width * lax.axis_size("tensor")
    squares = lax.psum(jnp.sum(residual * residual, axis=1), "tensor")
    normed = (residual * lax.rsqrt(squares[:, None] / full_width + EPSILON) * gain).astype(
        jnp.bfloat16
    )
    choosers = (routes[:, :, None] == jnp.arange(EXPERTS, dtype=jnp.int32)[None, None, :]).astype(
        jnp.int32
    )
    flat_choice = choosers.reshape(2 * local_seqs, EXPERTS)
    earlier = jnp.cumsum(flat_choice, axis=0) - flat_choice
    slot_index = jnp.sum(earlier * flat_choice, axis=1)
    target = (routes.reshape(-1) * CAP + slot_index).reshape(local_seqs, 2)
    devices = lax.axis_size("expert")
    per_expert = devices // EXPERTS
    packed = pack_slots(target, normed).reshape(EXPERTS, 1, CAP, local_width)
    outgoing = jnp.broadcast_to(packed, (EXPERTS, per_expert, CAP, local_width)).reshape(
        devices, CAP, local_width
    )
    arrived = lax.all_to_all(outgoing, "expert", split_axis=0, concat_axis=0, tiled=True)
    sources = arrived.shape[0]
    items = arrived.shape[1]
    produced = expert_hidden(
        arrived.reshape(sources * items, local_width), gate_weight, up_weight, down_weight
    )
    computed = produced.reshape(sources, items, local_width)
    returned = lax.all_to_all(computed, "expert", split_axis=0, concat_axis=0, tiled=True)
    per_slot = jnp.sum(returned.reshape(EXPERTS, per_expert, CAP, local_width), axis=1)
    moe_sum = mix_slots(target, route_weights, per_slot.reshape(EXPERTS * CAP, local_width))
    return (residual + moe_sum).astype(jnp.bfloat16)


MESH = pl.DeviceIdType.MESH
PAD = 16


def fused_kernel(
    dims,
    lengths_ref, routes_ref,
    tokens_hbm, queries_hbm, new_hbm, cache_hbm, gain_hbm, mixw_hbm,
    gate_hbm, up_hbm, down_hbm,
    out_ref,
    tok, qry, new, cache, gain, mixw, resid,
    ysend, arr, ss_send, ss_arr, ss_rows, ss_flat, flat, tall, xin,
    gate_w, up_w, down_w,
    part, got1, half16, half32, got2, hid, acc, ret_send, ret,
    in_sem, gate_sem, up_sem, down_sem,
    a2a_send, a2a_recv, sa_send, sa_recv, sr_send, sr_recv,
    s1_send, s1_recv, s2_send, s2_recv, h1_send, h1_recv, h2_send, h2_recv, h3_send, h3_recv,
    rt_send, rt_recv,
):
    seqs, heads, groups, hd, ctx, kvh, full_width, chunks, width, slots, rows = dims
    half, quarter = width // 2, width // 4
    p = lax.axis_index("parts")
    me = lax.axis_index("expert")
    t = lax.axis_index("tensor")
    core = lax.rem(t, 2)
    xpos = lax.div(t, 2)
    sibling = t + 1 - 2 * core
    across = lax.rem(t + 2, 4)
    diagonal = lax.rem(sibling + 2, 4)
    f32, bf16 = jnp.float32, jnp.bfloat16

    barrier = pltpu.get_barrier_semaphore()
    for j in range(1, EXPERTS):
        pl.semaphore_signal(barrier, inc=1, device_id=(p, lax.rem(me + j, EXPERTS), t), device_id_type=MESH)
    for other in (sibling, across, diagonal):
        pl.semaphore_signal(barrier, inc=1, device_id=(p, me, other), device_id_type=MESH)

    small = [
        pltpu.make_async_copy(a, b, in_sem.at[n])
        for n, (a, b) in enumerate(
            [(queries_hbm, qry), (cache_hbm, cache), (new_hbm, new), (tokens_hbm, tok), (gain_hbm, gain), (mixw_hbm, mixw)]
        )
    ]
    for cp in small:
        cp.start()
    flat[...] = jnp.zeros_like(flat)
    tall[...] = jnp.zeros_like(tall)
    ss_flat[...] = jnp.zeros_like(ss_flat)
    ss_send[...] = jnp.zeros_like(ss_send)

    def gate_copy(i):
        s = lax.rem(i, slots)
        cols = pl.ds(pl.multiple_of(i * width, width), width)
        return pltpu.make_async_copy(gate_hbm.at[:, cols], gate_w.at[s], gate_sem.at[s])

    def up_copy(i):
        s = lax.rem(i, slots)
        cols = pl.ds(pl.multiple_of(i * width, width), width)
        return pltpu.make_async_copy(up_hbm.at[:, cols], up_w.at[s], up_sem.at[s])

    def down_copy(i):
        rws = pl.ds(pl.multiple_of(i * width, width), width)
        return pltpu.make_async_copy(down_hbm.at[rws, :], down_w.at[i], down_sem.at[i])

    counts = [jnp.int32(0)] * EXPERTS
    targets = []
    for s in range(seqs):
        pair = []
        for j in range(2):
            k = routes_ref[j, s]
            idx = counts[0]
            for e in range(1, EXPERTS):
                idx = jnp.where(k == e, counts[e], idx)
            counts = [counts[e] + jnp.where(k == e, 1, 0) for e in range(EXPERTS)]
            pair.append(k * CAP + idx)
        targets.append(pair)
    prow = lax.broadcasted_iota(jnp.int32, (rows, seqs), 0)
    pcol = lax.broadcasted_iota(jnp.int32, (rows, seqs), 1)
    pt = [jnp.full((rows, seqs), -1, jnp.int32)] * 2
    for s in range(seqs):
        for j in range(2):
            pt[j] = jnp.where(pcol == s, targets[s][j], pt[j])
    placing = jnp.where((prow == pt[0]) | (prow == pt[1]), f32(1.0), f32(0.0))

    for cp in small:
        cp.wait()
    for i in range(slots):
        gate_copy(i).start()
        up_copy(i).start()
    q = qry[...].reshape(heads * seqs, hd)
    factor = 1.0 / math.sqrt(hd)
    dn = (((1,), (1,)), ((), ()))
    nq, nk, nn = heads * seqs, seqs * ctx * kvh, seqs * kvh
    s_old = lax.dot_general(q, cache[0], dn, preferred_element_type=f32) * factor
    s_new = lax.dot_general(q, new[0], dn, preferred_element_type=f32) * factor
    limit = jnp.zeros((1, nk), jnp.int32)
    kcol = lax.broadcasted_iota(jnp.int32, (1, nk), 1)
    for s in range(seqs):
        limit = jnp.where(kcol // (ctx * kvh) == s, lengths_ref[s], limit)
    kpos = (kcol // kvh) % ctx
    key_old = jnp.where(kpos < limit, (kcol // (ctx * kvh)) * kvh + kcol % kvh, -1)
    key_new = lax.broadcasted_iota(jnp.int32, (1, nn), 1)
    qrow = lax.broadcasted_iota(jnp.int32, (nq, 1), 0)
    key_q = (qrow % seqs) * kvh + qrow // (seqs * groups)
    low = f32(-1e30)
    s_old = jnp.where(key_q == key_old, s_old, low)
    s_new = jnp.where(key_q == key_new, s_new, low)
    largest = jnp.maximum(jnp.max(s_old, axis=1, keepdims=True), jnp.max(s_new, axis=1, keepdims=True))
    w_old = jnp.exp(s_old - largest)
    w_new = jnp.exp(s_new - largest)
    den = jnp.sum(w_old, axis=1, keepdims=True) + jnp.sum(w_new, axis=1, keepdims=True)
    p_old = (w_old / den).astype(bf16)
    p_new = (w_new / den).astype(bf16)
    att = jnp.dot(p_old, cache[1], preferred_element_type=f32) + jnp.dot(
        p_new, new[1], preferred_element_type=f32
    )
    squares = jnp.zeros((seqs, 1), f32)
    for h in range(heads):
        cols = slice(h * hd, (h + 1) * hd)
        piece = tok[:, cols].astype(f32) + att[h * seqs : (h + 1) * seqs]
        resid[:, cols] = piece
        squares = squares + jnp.sum(piece * piece, axis=1, keepdims=True)
    scaled = (resid[...] * gain[...].reshape(1, -1)).astype(bf16)
    flat[...] = jnp.dot(placing.astype(bf16), scaled, preferred_element_type=f32)
    fold(flat, tall, ysend)
    ss_flat[...] = jnp.dot(
        placing, jnp.broadcast_to(squares, (seqs, 128)),
        precision=lax.Precision.HIGHEST, preferred_element_type=f32,
    )
    for e in range(EXPERTS):
        ss_send[e, :CAP] = ss_flat[e * CAP : (e + 1) * CAP]
    pl.semaphore_wait(barrier, EXPERTS + 2)

    def exchange(src, dst, send, recv, j):
        to = lax.rem(me + j, EXPERTS)
        return pltpu.make_async_remote_copy(
            src_ref=src.at[to], dst_ref=dst.at[me], send_sem=send.at[j - 1], recv_sem=recv.at[j - 1],
            device_id=(p, to, t), device_id_type=MESH,
        )

    for j in (2, 3, 1):
        exchange(ysend, arr, a2a_send, a2a_recv, j).start()
    for j in (2, 3, 1):
        exchange(ss_send, ss_arr, sa_send, sa_recv, j).start()
    arr[me] = ysend[me]
    ss_arr[me] = ss_send[me]
    down_copy(0).start()
    for j in (1, 2, 3):
        exchange(ysend, arr, a2a_send, a2a_recv, j).wait()
    unfold(arr, tall, flat)
    xin[...] = flat[...].astype(bf16)

    def ss_copy(j):
        return pltpu.make_async_remote_copy(
            src_ref=ss_rows.at[t], dst_ref=ss_rows.at[t], send_sem=sr_send.at[j - 1], recv_sem=sr_recv.at[j - 1],
            device_id=(p, me, lax.rem(t + j, 4)), device_id_type=MESH,
        )

    acc[...] = jnp.zeros_like(acc)

    def remote(src, dst, send, recv, i, to):
        return pltpu.make_async_remote_copy(
            src_ref=src, dst_ref=dst, send_sem=send.at[i], recv_sem=recv.at[i],
            device_id=(p, me, to), device_id_type=MESH,
        )

    def at_half(c):
        return pl.ds(pl.multiple_of(c * half, half), half)

    def at_quarter(n):
        return pl.ds(pl.multiple_of(n * quarter, quarter), quarter)

    mine = core * 2 + xpos
    theirs = core * 2 + 1 - xpos

    def stage1(i):
        return remote(part.at[i, :, :, at_half(1 - core)], got1.at[i], s1_send, s1_recv, i, sibling)

    def stage2(i):
        return remote(half16.at[i, :, :, at_quarter(1 - xpos)], got2.at[i], s2_send, s2_recv, i, across)

    def spread1(i):
        return remote(hid.at[i, :, at_quarter(mine)], hid.at[i, :, at_quarter(mine)], h1_send, h1_recv, i, across)

    def spread2(i):
        return remote(hid.at[i, :, at_quarter(mine)], hid.at[i, :, at_quarter(mine)], h2_send, h2_recv, i, sibling)

    def spread3(i):
        return remote(hid.at[i, :, at_quarter(theirs)], hid.at[i, :, at_quarter(theirs)], h3_send, h3_recv, i, sibling)

    def exchange_squares():
        for j in (1, 2, 3):
            exchange(ss_send, ss_arr, sa_send, sa_recv, j).wait()
        for e in range(EXPERTS):
            ss_flat[e * CAP : (e + 1) * CAP] = ss_arr[e, :CAP]
        ss_rows[t] = ss_flat[...]
        for j in (1, 2, 3):
            ss_copy(j).start()

    def direct(i):
        return remote(hid.at[i, :, at_quarter(mine)], hid.at[i, :, at_quarter(mine)], h3_send, h3_recv, i, diagonal)

    def multiply(i):
        s = lax.rem(i, slots)
        gate_copy(i).wait()
        part[i, 0] = jnp.dot(xin[...], gate_w[s], preferred_element_type=f32).astype(bf16)
        pl.when(i == 0)(exchange_squares)
        up_copy(i).wait()
        part[i, 1] = jnp.dot(xin[...], up_w[s], preferred_element_type=f32).astype(bf16)
        stage1(i).start()

        @pl.when(i + slots < chunks)
        def _():
            gate_copy(i + slots).start()
            up_copy(i + slots).start()

        @pl.when(i + 1 < chunks)
        def _():
            down_copy(i + 1).start()

    def add_core(b):
        stage1(b).wait_recv()
        for n in range(2):
            both = part[b, n, :, at_half(core)].astype(f32) + got1[b, n].astype(f32)
            half32[b, n] = both
            half16[b, n] = both.astype(bf16)
        stage2(b).start()

    def activate(c):
        @pl.when(c == 0)
        def _():
            for j in (1, 2, 3):
                ss_copy(j).wait()
            ss_rows[t] = ss_rows[0] + ss_rows[1] + ss_rows[2] + ss_rows[3]

        stage2(c).wait_recv()
        scale = lax.rsqrt(ss_rows[t][:, :1] / full_width + EPSILON)
        g = (half32[c, 0, :, at_quarter(xpos)] + got2[c, 0].astype(f32)) * scale
        u = (half32[c, 1, :, at_quarter(xpos)] + got2[c, 1].astype(f32)) * scale
        hid[c, :, at_quarter(mine)] = (g / (1.0 + jnp.exp(-g)) * u).astype(bf16)
        spread1(c).start()
        spread2(c).start()

        @pl.when(c >= chunks - DIRECT)
        def _():
            direct(c).start()

    def hand_on(d):
        @pl.when(d < chunks - DIRECT)
        def _():
            spread1(d).wait_recv()
            spread3(d).start()

    def project(e):
        @pl.when(e >= chunks - DIRECT)
        def _():
            spread1(e).wait_recv()

        spread2(e).wait_recv()
        spread3(e).wait_recv()
        down_copy(e).wait()
        acc[...] += jnp.dot(hid[e], down_w[e], preferred_element_type=f32)

    def step(i, carry):
        multiply(i)
        pl.when(i >= 1)(lambda: add_core(i - 1))
        pl.when(i >= 3)(lambda: activate(i - 3))
        pl.when(i >= 5)(lambda: hand_on(i - 5))
        return carry

    lax.fori_loop(0, chunks, step, 0)

    def finish(u, carry):
        project(u)
        pl.when(u == 0)(lambda: add_core(u + chunks - 1))
        late = jnp.maximum(u - 1, 0)

        @pl.when((u == 0) | (u == 2) | (u == 3))
        def _():
            activate(late + chunks - 3)
            hand_on(late + chunks - 5)

        return carry

    lax.fori_loop(0, chunks, finish, 0)

    fold(acc, tall, ret_send)
    for j in (2, 3, 1):
        exchange(ret_send, ret, rt_send, rt_recv, j).start()
    ret[me] = ret_send[me]
    weights = mixw[...].astype(f32)
    mixing = jnp.where(prow == pt[0], weights[0:1], f32(0.0)) + jnp.where(prow == pt[1], weights[1:2], f32(0.0))

    def drain(i, carry):
        for copy in (stage1, stage2, spread1, spread2, spread3):
            copy(i).wait_send()
        return carry

    lax.fori_loop(0, chunks, drain, 0)
    for j in (1, 2, 3):
        exchange(ret_send, ret, rt_send, rt_recv, j).wait()
    unfold(ret, tall, flat)
    moe = lax.dot_general(
        mixing.astype(bf16), flat[...].astype(bf16), (((0,), (0,)), ((), ())),
        preferred_element_type=f32,
    )
    out_ref[...] = (resid[...] + moe).astype(bf16)


def fold(flat, tall, out):
    for e in range(EXPERTS):
        for j in range(flat.shape[1] // 128):
            tall[e, j * CAP : (j + 1) * CAP] = flat[e * CAP : (e + 1) * CAP, j * 128 : (j + 1) * 128]
        out[e] = tall[e].astype(out.dtype)


def unfold(src, tall, flat):
    for e in range(EXPERTS):
        tall[e] = src[e].astype(tall.dtype)
        for j in range(flat.shape[1] // 128):
            flat[e * CAP : (e + 1) * CAP, j * 128 : (j + 1) * 128] = tall[e, j * CAP : (j + 1) * CAP]


DIRECT = 2


def fused(
    tokens, queries, new_kv, cache_kv, lengths, gain, gate_weight, up_weight, down_weight, routes, route_weights
):
    seqs, width_in = tokens.shape
    heads, hd = queries.shape[1:]
    ctx, kvh = cache_kv.shape[2:4]
    ff = gate_weight.shape[1]
    width = min(1024, ff)
    chunks = ff // width
    slots = min(5, chunks)
    rows = -(-EXPERTS * CAP // 8) * 8
    full_width = width_in * lax.axis_size("tensor")
    dims = (seqs, heads, heads // kvh, hd, ctx, kvh, full_width, chunks, width, slots, rows)
    high = -(-(width_in // 128 * CAP) // 16) * 16
    half, quarter = width // 2, width // 4
    bf16, f32 = jnp.bfloat16, jnp.float32
    vm, dma = pltpu.VMEM, pltpu.SemaphoreType.DMA
    nk, nn = seqs * ctx * kvh, seqs * kvh
    scratch = [
        vm((seqs, width_in), bf16), vm((heads, seqs, hd), bf16), vm((2, nn, hd), bf16), vm((2, nk, hd), bf16),
        vm((width_in,), f32), vm((2, seqs), bf16), vm((seqs, width_in), f32),
        vm((EXPERTS, high, 128), bf16), vm((EXPERTS, high, 128), bf16),
        vm((EXPERTS, PAD, 128), f32), vm((EXPERTS, PAD, 128), f32), vm((4, rows, 128), f32),
        vm((rows, 128), f32), vm((rows, width_in), f32), vm((EXPERTS, high, 128), f32),
        vm((rows, width_in), bf16),
        vm((slots, width_in, width), bf16), vm((slots, width_in, width), bf16), vm((chunks, width, width_in), bf16),
        vm((chunks, 2, rows, width), bf16), vm((chunks, 2, rows, half), bf16),
        vm((chunks, 2, rows, half), bf16), vm((chunks, 2, rows, half), f32),
        vm((chunks, 2, rows, quarter), bf16), vm((chunks, rows, width), bf16),
        vm((rows, width_in), f32),
        vm((EXPERTS, high, 128), bf16), vm((EXPERTS, high, 128), bf16),
        dma((6,)), dma((slots,)), dma((slots,)), dma((chunks,)),
    ] + [dma((3,))] * 6 + [dma((chunks,))] * 10 + [dma((3,))] * 2
    smem = pl.BlockSpec(memory_space=pltpu.SMEM)
    anyspace = pl.BlockSpec(memory_space=pl.ANY)
    return pl.pallas_call(
        functools.partial(fused_kernel, dims),
        out_shape=jax.ShapeDtypeStruct((seqs, width_in), bf16),
        in_specs=[smem] * 2 + [anyspace] * 9,
        out_specs=pl.BlockSpec(memory_space=pltpu.VMEM),
        scratch_shapes=scratch,
        compiler_params=pltpu.CompilerParams(
            collective_id=0, has_side_effects=True, vmem_limit_bytes=67043328
        ),
    )(
        lengths, routes.T, tokens, jnp.transpose(queries, (1, 0, 2)), new_kv.reshape(2, nn, hd), cache_kv.reshape(2, nk, hd),
        gain, route_weights.T, gate_weight, up_weight, down_weight,
    )


def solution(mesh):
    in_specs = (
        P(("parts", "expert"), "tensor"),
        P(("parts", "expert"), "tensor", None),
        P(None, ("parts", "expert"), "tensor", None),
        P(None, ("parts", "expert"), None, "tensor", None),
        P(("parts", "expert")),
        P("tensor"),
        P("tensor", "expert"),
        P("tensor", "expert"),
        P("expert", "tensor"),
        P(("parts", "expert"), None),
        P(("parts", "expert"), None),
    )
    out_specs = P(("parts", "expert"), "tensor")
    square = mesh.shape["expert"] == EXPERTS and mesh.shape["tensor"] == 4

    def run(*args):
        wide = args[6].shape[1] >= 8 * 1024
        return (fused if square and wide else on_device)(*args)

    return jax.shard_map(
        run, mesh=mesh, in_specs=in_specs, out_specs=out_specs, check_vma=False
    )
```

profile of v0, /device:TPU:0, one launch (start us, length us, event | category | flops | bytes accessed | tf_op | source)
XLA Modules:
  0.0 40.3 jit_solution(2025356826579537391)
XLA Ops:
  0.0 38.9 %shard_map.109 = bf16[16,1536]{1,0:T(8,128)(2,1)} custom-call(s32[16]{0:T(128)} %lengths_ref.1, s32[2,16]{1,0:T(2,128)} %bitcast.8, bf16[16,1536]{1,0:T(8,128)(2,1)} %tokens_hbm.1, bf16[12,16,128]{2,1,0:T(8,128)(2,1)} %bitcast.6, bf16[2,32,128]{2,1,0:T(8,128)(2,1)} %bitcast.7, bf16[2,512,128]{2,1,0:T(8,128)(2,1)} %bitcast.5, f32[1536]{0:T(1024)} %gain_hbm.1, ...), custom_call_target="tpu_custom_call" | custom-call | tf_op jit(solution)/shard_map/pallas_call | solution.py:491
  38.9 1.4 %copy.13 = bf16[16,1536]{1,0:T(8,128)(2,1)} copy(bf16[16,1536]{1,0:T(8,128)(2,1)} %shard_map.109) | data formatting | bytes 98304
where the time goes:
time: 40.5 us; the launch traced here: 40.3 us
  Pallas kernels  38.9 us (96%)
  local copies, waits for them, and re-layouts  1.42 us (4%)
    pallas_call x1, Pallas kernels, fused(): pl.pallas_call(functools.partial(fused_kernel, dims), out_shape=jax.Shape...  38.9 us
    unnamed x1, local copies, waits for them, and re-layouts  1.42 us

commit v1 on v0

--- a/solution.py
+++ b/solution.py
@@ -128,25 +128,24 @@
 
 
 MESH = pl.DeviceIdType.MESH
-PAD = 16
 
 
 def fused_kernel(
     dims,
-    lengths_ref, routes_ref,
+    lengths_hbm, routes_hbm,
     tokens_hbm, queries_hbm, new_hbm, cache_hbm, gain_hbm, mixw_hbm,
     gate_hbm, up_hbm, down_hbm,
     out_ref,
-    tok, qry, new, cache, gain, mixw, resid,
-    ysend, arr, ss_send, ss_arr, ss_rows, ss_flat, flat, tall, xin,
+    lens, route, tok, qry, new, cache, gain, mixw, resid, mixt,
+    ysend, arr, ss_rows, flat, tall, xin,
     gate_w, up_w, down_w,
-    part, got1, half16, half32, got2, hid, acc, ret_send, ret,
+    part, got1, half16, half32, got2, hid, acc, rtall, ret_send, ret,
     in_sem, gate_sem, up_sem, down_sem,
-    a2a_send, a2a_recv, sa_send, sa_recv, sr_send, sr_recv,
+    a2a_send, a2a_recv, sr_send, sr_recv,
     s1_send, s1_recv, s2_send, s2_recv, h1_send, h1_recv, h2_send, h2_recv, h3_send, h3_recv,
     rt_send, rt_recv,
 ):
-    seqs, heads, groups, hd, ctx, kvh, full_width, chunks, width, slots, rows = dims
+    seqs, heads, groups, hd, ctx, kvh, full_width, chunks, width, slots, rows, blocks = dims
     half, quarter = width // 2, width // 4
     p = lax.axis_index("parts")
     me = lax.axis_index("expert")
@@ -167,15 +166,14 @@
     small = [
         pltpu.make_async_copy(a, b, in_sem.at[n])
         for n, (a, b) in enumerate(
-            [(queries_hbm, qry), (cache_hbm, cache), (new_hbm, new), (tokens_hbm, tok), (gain_hbm, gain), (mixw_hbm, mixw)]
+            [
+                (queries_hbm, qry), (cache_hbm, cache), (new_hbm, new), (lengths_hbm, lens), (routes_hbm, route),
+                (tokens_hbm, tok), (gain_hbm, gain), (mixw_hbm, mixw),
+            ]
         )
     ]
     for cp in small:
         cp.start()
-    flat[...] = jnp.zeros_like(flat)
-    tall[...] = jnp.zeros_like(tall)
-    ss_flat[...] = jnp.zeros_like(ss_flat)
-    ss_send[...] = jnp.zeros_like(ss_send)
 
     def gate_copy(i):
         s = lax.rem(i, slots)
@@ -191,43 +189,47 @@
         rws = pl.ds(pl.multiple_of(i * width, width), width)
         return pltpu.make_async_copy(down_hbm.at[rws, :], down_w.at[i], down_sem.at[i])
 
-    counts = [jnp.int32(0)] * EXPERTS
-    targets = []
-    for s in range(seqs):
-        pair = []
-        for j in range(2):
-            k = routes_ref[j, s]
-            idx = counts[0]
-            for e in range(1, EXPERTS):
-                idx = jnp.where(k == e, counts[e], idx)
-            counts = [counts[e] + jnp.where(k == e, 1, 0) for e in range(EXPERTS)]
-            pair.append(k * CAP + idx)
-        targets.append(pair)
-    prow = lax.broadcasted_iota(jnp.int32, (rows, seqs), 0)
-    pcol = lax.broadcasted_iota(jnp.int32, (rows, seqs), 1)
-    pt = [jnp.full((rows, seqs), -1, jnp.int32)] * 2
-    for s in range(seqs):
-        for j in range(2):
-            pt[j] = jnp.where(pcol == s, targets[s][j], pt[j])
-    placing = jnp.where((prow == pt[0]) | (prow == pt[1]), f32(1.0), f32(0.0))
-
+    for i in range(2):
+        gate_copy(i).start(priority=1)
+        up_copy(i).start(priority=1)
+    tall[...] = jnp.zeros_like(tall)
+    rtall[...] = jnp.zeros_like(rtall)
+    acc[...] = jnp.zeros_like(acc)
     for cp in small:
         cp.wait()
-    for i in range(slots):
-        gate_copy(i).start()
-        up_copy(i).start()
+
+    prow = lax.broadcasted_iota(jnp.int32, (rows, seqs), 0)
+    expert_of = sum((prow >= e * CAP).astype(jnp.int32) for e in range(1, EXPERTS + 1))
+    picks = [route[j : j + 1, :] == expert_of for j in range(2)]
+    named = jnp.where(picks[0] | picks[1], f32(1.0), f32(0.0))
+    earlier = lax.broadcasted_iota(jnp.int32, (seqs, seqs), 0) < lax.broadcasted_iota(jnp.int32, (seqs, seqs), 1)
+    before = jnp.dot(
+        named.astype(bf16), jnp.where(earlier, f32(1.0), f32(0.0)).astype(bf16), preferred_element_type=f32
+    )
+    slot_of = (prow - expert_of * CAP).astype(f32)
+    placing = jnp.where(before == slot_of, named, f32(0.0))
+    weights = mixw[...].astype(f32)
+    mixing = placing * jnp.where(picks[0], weights[0:1], weights[1:2])
+    same = lax.broadcasted_iota(jnp.int32, (seqs, seqs), 0) == lax.broadcasted_iota(jnp.int32, (seqs, seqs), 1)
+    mixt[...] = lax.dot_general(
+        jnp.where(same, f32(1.0), f32(0.0)).astype(bf16), mixing.astype(bf16), (((1,), (1,)), ((), ())),
+        preferred_element_type=f32,
+    ).astype(bf16)
     q = qry[...].reshape(heads * seqs, hd)
     factor = 1.0 / math.sqrt(hd)
     dn = (((1,), (1,)), ((), ()))
     nq, nk, nn = heads * seqs, seqs * ctx * kvh, seqs * kvh
     s_old = lax.dot_general(q, cache[0], dn, preferred_element_type=f32) * factor
     s_new = lax.dot_general(q, new[0], dn, preferred_element_type=f32) * factor
-    limit = jnp.zeros((1, nk), jnp.int32)
     kcol = lax.broadcasted_iota(jnp.int32, (1, nk), 1)
-    for s in range(seqs):
-        limit = jnp.where(kcol // (ctx * kvh) == s, lengths_ref[s], limit)
+    owner = lax.broadcasted_iota(jnp.int32, (seqs, nk), 0)
+    spread = lax.broadcasted_iota(jnp.int32, (seqs, nk), 1) // (ctx * kvh) == owner
+    limit = jnp.dot(
+        lens[...].astype(f32).astype(bf16), jnp.where(spread, f32(1.0), f32(0.0)).astype(bf16),
+        preferred_element_type=f32,
+    )
     kpos = (kcol // kvh) % ctx
-    key_old = jnp.where(kpos < limit, (kcol // (ctx * kvh)) * kvh + kcol % kvh, -1)
+    key_old = jnp.where(kpos.astype(f32) < limit, (kcol // (ctx * kvh)) * kvh + kcol % kvh, -1)
     key_new = lax.broadcasted_iota(jnp.int32, (1, nn), 1)
     qrow = lax.broadcasted_iota(jnp.int32, (nq, 1), 0)
     key_q = (qrow % seqs) * kvh + qrow // (seqs * groups)
@@ -243,21 +245,16 @@
     att = jnp.dot(p_old, cache[1], preferred_element_type=f32) + jnp.dot(
         p_new, new[1], preferred_element_type=f32
     )
-    squares = jnp.zeros((seqs, 1), f32)
     for h in range(heads):
         cols = slice(h * hd, (h + 1) * hd)
         piece = tok[:, cols].astype(f32) + att[h * seqs : (h + 1) * seqs]
         resid[:, cols] = piece
-        squares = squares + jnp.sum(piece * piece, axis=1, keepdims=True)
     scaled = (resid[...] * gain[...].reshape(1, -1)).astype(bf16)
     flat[...] = jnp.dot(placing.astype(bf16), scaled, preferred_element_type=f32)
     fold(flat, tall, ysend)
-    ss_flat[...] = jnp.dot(
-        placing, jnp.broadcast_to(squares, (seqs, 128)),
-        precision=lax.Precision.HIGHEST, preferred_element_type=f32,
-    )
-    for e in range(EXPERTS):
-        ss_send[e, :CAP] = ss_flat[e * CAP : (e + 1) * CAP]
+    for i in range(2, slots):
+        gate_copy(i).start(priority=1)
+        up_copy(i).start(priority=1)
     pl.semaphore_wait(barrier, EXPERTS + 2)
 
     def exchange(src, dst, send, recv, j):
@@ -269,11 +266,7 @@
 
     for j in (2, 3, 1):
         exchange(ysend, arr, a2a_send, a2a_recv, j).start()
-    for j in (2, 3, 1):
-        exchange(ss_send, ss_arr, sa_send, sa_recv, j).start()
     arr[me] = ysend[me]
-    ss_arr[me] = ss_send[me]
-    down_copy(0).start()
     for j in (1, 2, 3):
         exchange(ysend, arr, a2a_send, a2a_recv, j).wait()
     unfold(arr, tall, flat)
@@ -285,8 +278,6 @@
             device_id=(p, me, lax.rem(t + j, 4)), device_id_type=MESH,
         )
 
-    acc[...] = jnp.zeros_like(acc)
-
     def remote(src, dst, send, recv, i, to):
         return pltpu.make_async_remote_copy(
             src_ref=src, dst_ref=dst, send_sem=send.at[i], recv_sem=recv.at[i],
@@ -318,11 +309,8 @@
         return remote(hid.at[i, :, at_quarter(theirs)], hid.at[i, :, at_quarter(theirs)], h3_send, h3_recv, i, sibling)
 
     def exchange_squares():
-        for j in (1, 2, 3):
-            exchange(ss_send, ss_arr, sa_send, sa_recv, j).wait()
-        for e in range(EXPERTS):
-            ss_flat[e * CAP : (e + 1) * CAP] = ss_arr[e, :CAP]
-        ss_rows[t] = ss_flat[...]
+        raw = flat[...] * (1.0 / gain[...].reshape(1, -1))
+        ss_rows[t] = jnp.broadcast_to(jnp.sum(raw * raw, axis=1, keepdims=True), (rows, 128))
         for j in (1, 2, 3):
             ss_copy(j).start()
 
@@ -333,19 +321,18 @@
         s = lax.rem(i, slots)
         gate_copy(i).wait()
         part[i, 0] = jnp.dot(xin[...], gate_w[s], preferred_element_type=f32).astype(bf16)
-        pl.when(i == 0)(exchange_squares)
         up_copy(i).wait()
         part[i, 1] = jnp.dot(xin[...], up_w[s], preferred_element_type=f32).astype(bf16)
         stage1(i).start()
+        pl.when(i == 0)(exchange_squares)
 
         @pl.when(i + slots < chunks)
         def _():
-            gate_copy(i + slots).start()
-            up_copy(i + slots).start()
-
-        @pl.when(i + 1 < chunks)
-        def _():
-            down_copy(i + 1).start()
+            gate_copy(i + slots).start(priority=1)
+            up_copy(i + slots).start(priority=1)
+
+        for n in (2 * (i - chunks + slots) - 1, 2 * (i - chunks + slots)):
+            pl.when((n >= 0) & (n < chunks))(lambda n=n: down_copy(n).start(priority=1))
 
     def add_core(b):
         stage1(b).wait_recv()
@@ -380,7 +367,7 @@
             spread1(d).wait_recv()
             spread3(d).start()
 
-    def project(e):
+    def ready(e):
         @pl.when(e >= chunks - DIRECT)
         def _():
             spread1(e).wait_recv()
@@ -388,6 +375,9 @@
         spread2(e).wait_recv()
         spread3(e).wait_recv()
         down_copy(e).wait()
+
+    def project(e):
+        ready(e)
         acc[...] += jnp.dot(hid[e], down_w[e], preferred_element_type=f32)
 
     def step(i, carry):
@@ -411,14 +401,25 @@
 
         return carry
 
-    lax.fori_loop(0, chunks, finish, 0)
-
-    fold(acc, tall, ret_send)
-    for j in (2, 3, 1):
-        exchange(ret_send, ret, rt_send, rt_recv, j).start()
-    ret[me] = ret_send[me]
-    weights = mixw[...].astype(f32)
-    mixing = jnp.where(prow == pt[0], weights[0:1], f32(0.0)) + jnp.where(prow == pt[1], weights[1:2], f32(0.0))
+    lax.fori_loop(0, chunks - 1, finish, 0)
+
+    def give(b, j):
+        to = lax.rem(me + j, EXPERTS)
+        return pltpu.make_async_remote_copy(
+            src_ref=ret_send.at[b, to], dst_ref=ret.at[b, me], send_sem=rt_send.at[b, j - 1], recv_sem=rt_recv.at[b, j - 1],
+            device_id=(p, to, t), device_id_type=MESH,
+        )
+
+    last = chunks - 1
+    wide = acc.shape[1] // blocks
+    ready(last)
+    for b in range(blocks):
+        cols = slice(b * wide, (b + 1) * wide)
+        acc[:, cols] += jnp.dot(hid[last], down_w[last, :, cols], preferred_element_type=f32)
+        fold(acc.at[:, cols], rtall, ret_send.at[b])
+        for j in (2, 3, 1):
+            give(b, j).start()
+        ret[b, me] = ret_send[b, me]
 
     def drain(i, carry):
         for copy in (stage1, stage2, spread1, spread2, spread3):
@@ -426,14 +427,13 @@
         return carry
 
     lax.fori_loop(0, chunks, drain, 0)
-    for j in (1, 2, 3):
-        exchange(ret_send, ret, rt_send, rt_recv, j).wait()
-    unfold(ret, tall, flat)
-    moe = lax.dot_general(
-        mixing.astype(bf16), flat[...].astype(bf16), (((0,), (0,)), ((), ())),
-        preferred_element_type=f32,
-    )
-    out_ref[...] = (resid[...] + moe).astype(bf16)
+    for b in range(blocks):
+        cols = slice(b * wide, (b + 1) * wide)
+        for j in (1, 2, 3):
+            give(b, j).wait()
+        unfold(ret.at[b], rtall, flat.at[:, cols])
+        moe = jnp.dot(mixt[...], flat[:, cols].astype(bf16), preferred_element_type=f32)
+        out_ref[:, cols] = (resid[:, cols] + moe).astype(bf16)
 
 
 def fold(flat, tall, out):
@@ -465,40 +465,41 @@
     slots = min(5, chunks)
     rows = -(-EXPERTS * CAP // 8) * 8
     full_width = width_in * lax.axis_size("tensor")
-    dims = (seqs, heads, heads // kvh, hd, ctx, kvh, full_width, chunks, width, slots, rows)
+    blocks = 2
+    dims = (seqs, heads, heads // kvh, hd, ctx, kvh, full_width, chunks, width, slots, rows, blocks)
+    low = -(-(width_in // 128 // blocks * CAP) // 8) * 8
     high = -(-(width_in // 128 * CAP) // 16) * 16
     half, quarter = width // 2, width // 4
     bf16, f32 = jnp.bfloat16, jnp.float32
     vm, dma = pltpu.VMEM, pltpu.SemaphoreType.DMA
     nk, nn = seqs * ctx * kvh, seqs * kvh
     scratch = [
+        vm((1, seqs), jnp.int32), vm((2, seqs), jnp.int32),
         vm((seqs, width_in), bf16), vm((heads, seqs, hd), bf16), vm((2, nn, hd), bf16), vm((2, nk, hd), bf16),
-        vm((width_in,), f32), vm((2, seqs), bf16), vm((seqs, width_in), f32),
+        vm((width_in,), f32), vm((2, seqs), bf16), vm((seqs, width_in), f32), vm((seqs, rows), bf16),
         vm((EXPERTS, high, 128), bf16), vm((EXPERTS, high, 128), bf16),
-        vm((EXPERTS, PAD, 128), f32), vm((EXPERTS, PAD, 128), f32), vm((4, rows, 128), f32),
-        vm((rows, 128), f32), vm((rows, width_in), f32), vm((EXPERTS, high, 128), f32),
+        vm((4, rows, 128), f32), vm((rows, width_in), f32), vm((EXPERTS, high, 128), f32),
         vm((rows, width_in), bf16),
         vm((slots, width_in, width), bf16), vm((slots, width_in, width), bf16), vm((chunks, width, width_in), bf16),
         vm((chunks, 2, rows, width), bf16), vm((chunks, 2, rows, half), bf16),
         vm((chunks, 2, rows, half), bf16), vm((chunks, 2, rows, half), f32),
         vm((chunks, 2, rows, quarter), bf16), vm((chunks, rows, width), bf16),
-        vm((rows, width_in), f32),
-        vm((EXPERTS, high, 128), bf16), vm((EXPERTS, high, 128), bf16),
-        dma((6,)), dma((slots,)), dma((slots,)), dma((chunks,)),
-    ] + [dma((3,))] * 6 + [dma((chunks,))] * 10 + [dma((3,))] * 2
-    smem = pl.BlockSpec(memory_space=pltpu.SMEM)
+        vm((rows, width_in), f32), vm((EXPERTS, low, 128), f32),
+        vm((blocks, EXPERTS, low, 128), bf16), vm((blocks, EXPERTS, low, 128), bf16),
+        dma((8,)), dma((slots,)), dma((slots,)), dma((chunks,)),
+    ] + [dma((3,))] * 4 + [dma((chunks,))] * 10 + [dma((blocks, 3))] * 2
     anyspace = pl.BlockSpec(memory_space=pl.ANY)
     return pl.pallas_call(
         functools.partial(fused_kernel, dims),
         out_shape=jax.ShapeDtypeStruct((seqs, width_in), bf16),
-        in_specs=[smem] * 2 + [anyspace] * 9,
+        in_specs=[anyspace] * 11,
         out_specs=pl.BlockSpec(memory_space=pltpu.VMEM),
         scratch_shapes=scratch,
         compiler_params=pltpu.CompilerParams(
             collective_id=0, has_side_effects=True, vmem_limit_bytes=67043328
         ),
     )(
-        lengths, routes.T, tokens, jnp.transpose(queries, (1, 0, 2)), new_kv.reshape(2, nn, hd), cache_kv.reshape(2, nk, hd),
+        lengths.reshape(1, seqs), routes.T, tokens, jnp.transpose(queries, (1, 0, 2)), new_kv.reshape(2, nn, hd), cache_kv.reshape(2, nk, hd),
         gain, route_weights.T, gate_weight, up_weight, down_weight,
     )
 

time: 40.5 us -> 37.5 us (0.926)
  Pallas kernels: 38.9 us -> 35.9 us
    pallas_call x1, Pallas kernels: 38.9 us -> 35.9 us  [fused(): pl.pallas_call(functools.partial(fused_kernel, dims), out_shape=jax.Shape...]
where the time goes in v1:
time: 37.5 us; the launch traced here: 37.4 us
  Pallas kernels  35.9 us (96%)
  local copies, waits for them, and re-layouts  1.42 us (4%)
    pallas_call x1, Pallas kernels, fused(): pl.pallas_call(functools.partial(fused_kernel, dims), out_shape=jax.Shape...  35.9 us
    unnamed x1, local copies, waits for them, and re-layouts  1.42 us

profile of v1, /device:TPU:0, one launch (start us, length us, event | category | flops | bytes accessed | tf_op | source)
XLA Modules:
  0.0 37.4 jit_solution(14822878290676877296)
XLA Ops:
  0.0 35.9 %shard_map.109 = bf16[16,1536]{1,0:T(8,128)(2,1)} custom-call(s32[1,16]{1,0:T(1,128)} %bitcast.10, s32[2,16]{1,0:T(2,128)} %bitcast.9, bf16[16,1536]{1,0:T(8,128)(2,1)} %tokens_hbm.1, bf16[12,16,128]{2,1,0:T(8,128)(2,1)} %bitcast.7, bf16[2,32,128]{2,1,0:T(8,128)(2,1)} %bitcast.8, bf16[2,512,128]{2,1,0:T(8,128)(2,1)} %bitcast.6, f32[1536]{0:T(1024)} %gain_hbm.1, ...), custom_call_target="tpu_custom_call" | custom-call | tf_op jit(solution)/shard_map/pallas_call | solution.py:492
  35.9 1.4 %copy.13 = bf16[16,1536]{1,0:T(8,128)(2,1)} copy(bf16[16,1536]{1,0:T(8,128)(2,1)} %shard_map.109) | data formatting | bytes 98304

commit v2 on v1

--- a/solution.py
+++ b/solution.py
@@ -137,13 +137,11 @@
     gate_hbm, up_hbm, down_hbm,
     out_ref,
     lens, route, tok, qry, new, cache, gain, mixw, resid, mixt,
-    ysend, arr, ss_rows, flat, tall, xin,
-    gate_w, up_w, down_w,
+    ysend, arr, ss_rows, flat, tall,
+    lift_w, down_w,
     part, got1, half16, half32, got2, hid, acc, rtall, ret_send, ret,
-    in_sem, gate_sem, up_sem, down_sem,
-    a2a_send, a2a_recv, sr_send, sr_recv,
-    s1_send, s1_recv, s2_send, s2_recv, h1_send, h1_recv, h2_send, h2_recv, h3_send, h3_recv,
-    rt_send, rt_recv,
+    in_sem, lift_sem, down_sem, sent, a2a_recv, sr_recv,
+    s1_recv, s2_recv, h1_recv, h2_recv, rt_recv,
 ):
     seqs, heads, groups, hd, ctx, kvh, full_width, chunks, width, slots, rows, blocks = dims
     half, quarter = width // 2, width // 4
@@ -153,15 +151,16 @@
     core = lax.rem(t, 2)
     xpos = lax.div(t, 2)
     sibling = t + 1 - 2 * core
-    across = lax.rem(t + 2, 4)
-    diagonal = lax.rem(sibling + 2, 4)
+    partner = lax.rem(sibling + 2, 4)
+    other = lax.rem(t + 2, 4)
+    own = lax.rem(core + xpos, 2)
     f32, bf16 = jnp.float32, jnp.bfloat16
 
     barrier = pltpu.get_barrier_semaphore()
     for j in range(1, EXPERTS):
         pl.semaphore_signal(barrier, inc=1, device_id=(p, lax.rem(me + j, EXPERTS), t), device_id_type=MESH)
-    for other in (sibling, across, diagonal):
-        pl.semaphore_signal(barrier, inc=1, device_id=(p, me, other), device_id_type=MESH)
+    for peer in (sibling, partner, other):
+        pl.semaphore_signal(barrier, inc=1, device_id=(p, me, peer), device_id_type=MESH)
 
     small = [
         pltpu.make_async_copy(a, b, in_sem.at[n])
@@ -176,17 +175,17 @@
         cp.start()
 
     def gate_copy(i):
-        s = lax.rem(i, slots)
-        cols = pl.ds(pl.multiple_of(i * width, width), width)
-        return pltpu.make_async_copy(gate_hbm.at[:, cols], gate_w.at[s], gate_sem.at[s])
+        s = i % slots
+        cols = pl.ds(i * width, width)
+        return pltpu.make_async_copy(gate_hbm.at[:, cols], lift_w.at[s, 0], lift_sem.at[s])
 
     def up_copy(i):
-        s = lax.rem(i, slots)
-        cols = pl.ds(pl.multiple_of(i * width, width), width)
-        return pltpu.make_async_copy(up_hbm.at[:, cols], up_w.at[s], up_sem.at[s])
+        s = i % slots
+        cols = pl.ds(i * width, width)
+        return pltpu.make_async_copy(up_hbm.at[:, cols], lift_w.at[s, 1], lift_sem.at[s])
 
     def down_copy(i):
-        rws = pl.ds(pl.multiple_of(i * width, width), width)
+        rws = pl.ds(i * width, width)
         return pltpu.make_async_copy(down_hbm.at[rws, :], down_w.at[i], down_sem.at[i])
 
     for i in range(2):
@@ -257,30 +256,28 @@
         up_copy(i).start(priority=1)
     pl.semaphore_wait(barrier, EXPERTS + 2)
 
-    def exchange(src, dst, send, recv, j):
+    def exchange(j):
         to = lax.rem(me + j, EXPERTS)
         return pltpu.make_async_remote_copy(
-            src_ref=src.at[to], dst_ref=dst.at[me], send_sem=send.at[j - 1], recv_sem=recv.at[j - 1],
+            src_ref=ysend.at[to], dst_ref=arr.at[me], send_sem=sent.at[0], recv_sem=a2a_recv.at[0],
             device_id=(p, to, t), device_id_type=MESH,
         )
 
     for j in (2, 3, 1):
-        exchange(ysend, arr, a2a_send, a2a_recv, j).start()
+        exchange(j).start()
     arr[me] = ysend[me]
-    for j in (1, 2, 3):
-        exchange(ysend, arr, a2a_send, a2a_recv, j).wait()
+    landed(arr.at[pl.ds(0, EXPERTS - 1)], a2a_recv.at[0])
     unfold(arr, tall, flat)
-    xin[...] = flat[...].astype(bf16)
 
     def ss_copy(j):
         return pltpu.make_async_remote_copy(
-            src_ref=ss_rows.at[t], dst_ref=ss_rows.at[t], send_sem=sr_send.at[j - 1], recv_sem=sr_recv.at[j - 1],
+            src_ref=ss_rows.at[t], dst_ref=ss_rows.at[t], send_sem=sent.at[1], recv_sem=sr_recv.at[0],
             device_id=(p, me, lax.rem(t + j, 4)), device_id_type=MESH,
         )
 
-    def remote(src, dst, send, recv, i, to):
+    def remote(src, dst, n, recv, i, to):
         return pltpu.make_async_remote_copy(
-            src_ref=src, dst_ref=dst, send_sem=send.at[i], recv_sem=recv.at[i],
+            src_ref=src, dst_ref=dst, send_sem=sent.at[n], recv_sem=recv.at[i],
             device_id=(p, me, to), device_id_type=MESH,
         )
 
@@ -290,23 +287,23 @@
     def at_quarter(n):
         return pl.ds(pl.multiple_of(n * quarter, quarter), quarter)
 
-    mine = core * 2 + xpos
-    theirs = core * 2 + 1 - xpos
+    mine = own * 2 + xpos
+    theirs = own * 2 + 1 - xpos
 
     def stage1(i):
-        return remote(part.at[i, :, :, at_half(1 - core)], got1.at[i], s1_send, s1_recv, i, sibling)
+        return remote(part.at[i, :, :, at_half(1 - own)], got1.at[i], 2, s1_recv, i, sibling)
 
     def stage2(i):
-        return remote(half16.at[i, :, :, at_quarter(1 - xpos)], got2.at[i], s2_send, s2_recv, i, across)
+        return remote(half16.at[i, :, :, at_quarter(1 - xpos)], got2.at[i], 3, s2_recv, i, partner)
 
     def spread1(i):
-        return remote(hid.at[i, :, at_quarter(mine)], hid.at[i, :, at_quarter(mine)], h1_send, h1_recv, i, across)
+        return remote(hid.at[i, :, at_quarter(mine)], hid.at[i, :, at_quarter(mine)], 4, h1_recv, i, partner)
 
     def spread2(i):
-        return remote(hid.at[i, :, at_quarter(mine)], hid.at[i, :, at_quarter(mine)], h2_send, h2_recv, i, sibling)
+        return remote(hid.at[i, :, at_quarter(mine)], hid.at[i, :, at_quarter(mine)], 5, h2_recv, i, sibling)
 
     def spread3(i):
-        return remote(hid.at[i, :, at_quarter(theirs)], hid.at[i, :, at_quarter(theirs)], h3_send, h3_recv, i, sibling)
+        return remote(hid.at[i, :, at_quarter(theirs)], hid.at[i, :, at_quarter(theirs)], 6, h2_recv, i, sibling)
 
     def exchange_squares():
         raw = flat[...] * (1.0 / gain[...].reshape(1, -1))
@@ -315,40 +312,38 @@
             ss_copy(j).start()
 
     def direct(i):
-        return remote(hid.at[i, :, at_quarter(mine)], hid.at[i, :, at_quarter(mine)], h3_send, h3_recv, i, diagonal)
+        return remote(hid.at[i, :, at_quarter(mine)], hid.at[i, :, at_quarter(mine)], 6, h2_recv, i, other)
 
     def multiply(i):
-        s = lax.rem(i, slots)
-        gate_copy(i).wait()
-        part[i, 0] = jnp.dot(xin[...], gate_w[s], preferred_element_type=f32).astype(bf16)
-        up_copy(i).wait()
-        part[i, 1] = jnp.dot(xin[...], up_w[s], preferred_element_type=f32).astype(bf16)
+        s = i % slots
+        pltpu.make_async_copy(lift_w.at[s], lift_w.at[s], lift_sem.at[s]).wait()
+        part[i, 0] = jnp.dot(flat[...], lift_w[s, 0], preferred_element_type=f32).astype(bf16)
+        part[i, 1] = jnp.dot(flat[...], lift_w[s, 1], preferred_element_type=f32).astype(bf16)
         stage1(i).start()
-        pl.when(i == 0)(exchange_squares)
-
-        @pl.when(i + slots < chunks)
-        def _():
+        when(i == 0, exchange_squares)
+
+        if i + slots < chunks:
             gate_copy(i + slots).start(priority=1)
             up_copy(i + slots).start(priority=1)
-
         for n in (2 * (i - chunks + slots) - 1, 2 * (i - chunks + slots)):
-            pl.when((n >= 0) & (n < chunks))(lambda n=n: down_copy(n).start(priority=1))
+            if 0 <= n < chunks:
+                down_copy(n).start(priority=1)
 
     def add_core(b):
         stage1(b).wait_recv()
         for n in range(2):
-            both = part[b, n, :, at_half(core)].astype(f32) + got1[b, n].astype(f32)
+            both = part[b, n, :, at_half(own)].astype(f32) + got1[b, n].astype(f32)
             half32[b, n] = both
             half16[b, n] = both.astype(bf16)
         stage2(b).start()
 
     def activate(c):
-        @pl.when(c == 0)
-        def _():
-            for j in (1, 2, 3):
-                ss_copy(j).wait()
+        def total():
+            landed(ss_rows.at[pl.ds(0, 3)], sr_recv.at[0])
+            landed(ss_rows.at[pl.ds(0, 3)], sent.at[1])
             ss_rows[t] = ss_rows[0] + ss_rows[1] + ss_rows[2] + ss_rows[3]
 
+        when(c == 0, total)
         stage2(c).wait_recv()
         scale = lax.rsqrt(ss_rows[t][:, :1] / full_width + EPSILON)
         g = (half32[c, 0, :, at_quarter(xpos)] + got2[c, 0].astype(f32)) * scale
@@ -357,60 +352,56 @@
         spread1(c).start()
         spread2(c).start()
 
-        @pl.when(c >= chunks - DIRECT)
-        def _():
-            direct(c).start()
+        when(c >= chunks - DIRECT, lambda: direct(c).start())
 
     def hand_on(d):
-        @pl.when(d < chunks - DIRECT)
-        def _():
+        def pass_on():
             spread1(d).wait_recv()
             spread3(d).start()
 
+        when(d < chunks - DIRECT, pass_on)
+
     def ready(e):
-        @pl.when(e >= chunks - DIRECT)
-        def _():
-            spread1(e).wait_recv()
-
-        spread2(e).wait_recv()
-        spread3(e).wait_recv()
+        when(e >= chunks - DIRECT, lambda: spread1(e).wait_recv())
+        landed(hid.at[e, :, pl.ds(0, half)], h2_recv.at[e])
         down_copy(e).wait()
 
     def project(e):
         ready(e)
         acc[...] += jnp.dot(hid[e], down_w[e], preferred_element_type=f32)
 
-    def step(i, carry):
+    for i in range(chunks):
         multiply(i)
-        pl.when(i >= 1)(lambda: add_core(i - 1))
-        pl.when(i >= 3)(lambda: activate(i - 3))
-        pl.when(i >= 5)(lambda: hand_on(i - 5))
-        return carry
-
-    lax.fori_loop(0, chunks, step, 0)
-
-    def finish(u, carry):
-        project(u)
-        pl.when(u == 0)(lambda: add_core(u + chunks - 1))
-        late = jnp.maximum(u - 1, 0)
-
-        @pl.when((u == 0) | (u == 2) | (u == 3))
-        def _():
-            activate(late + chunks - 3)
-            hand_on(late + chunks - 5)
-
-        return carry
-
-    lax.fori_loop(0, chunks - 1, finish, 0)
+        when(i >= 1, lambda: add_core(i - 1))
+        when(i >= 4, lambda: activate(i - 4))
+        when(i >= 7, lambda: hand_on(i - 7))
+
+    last = chunks - 1
+    activate(last - 3)
+    add_core(last)
+    hand_on(last - 6)
+    project(last - 7)
+    hand_on(last - 5)
+    activate(last - 2)
+    project(last - 6)
+    hand_on(last - 4)
+    activate(last - 1)
+    project(last - 5)
+    hand_on(last - 3)
+    activate(last)
+    project(last - 4)
+    hand_on(last - 2)
+    project(last - 3)
+    project(last - 2)
+    project(last - 1)
 
     def give(b, j):
         to = lax.rem(me + j, EXPERTS)
         return pltpu.make_async_remote_copy(
-            src_ref=ret_send.at[b, to], dst_ref=ret.at[b, me], send_sem=rt_send.at[b, j - 1], recv_sem=rt_recv.at[b, j - 1],
+            src_ref=ret_send.at[b, to], dst_ref=ret.at[b, me], send_sem=sent.at[7], recv_sem=rt_recv.at[b],
             device_id=(p, to, t), device_id_type=MESH,
         )
 
-    last = chunks - 1
     wide = acc.shape[1] // blocks
     ready(last)
     for b in range(blocks):
@@ -421,19 +412,27 @@
             give(b, j).start()
         ret[b, me] = ret_send[b, me]
 
-    def drain(i, carry):
-        for copy in (stage1, stage2, spread1, spread2, spread3):
-            copy(i).wait_send()
-        return carry
-
-    lax.fori_loop(0, chunks, drain, 0)
+    landed(arr.at[pl.ds(0, EXPERTS - 1)], sent.at[0])
+    landed(got1, sent.at[2])
+    landed(got2, sent.at[3])
+    for n in (4, 5, 6):
+        landed(hid.at[:, :, pl.ds(0, quarter)], sent.at[n])
     for b in range(blocks):
         cols = slice(b * wide, (b + 1) * wide)
-        for j in (1, 2, 3):
-            give(b, j).wait()
+        landed(ret.at[b, pl.ds(0, EXPERTS - 1)], rt_recv.at[b])
         unfold(ret.at[b], rtall, flat.at[:, cols])
         moe = jnp.dot(mixt[...], flat[:, cols].astype(bf16), preferred_element_type=f32)
         out_ref[:, cols] = (resid[:, cols] + moe).astype(bf16)
+    landed(ret.at[:, pl.ds(0, EXPERTS - 1)], sent.at[7])
+
+
+def when(condition, run):
+    if condition:
+        run()
+
+
+def landed(ref, sem):
+    pltpu.make_async_copy(ref, ref, sem).wait()
 
 
 def fold(flat, tall, out):
@@ -479,24 +478,23 @@
         vm((width_in,), f32), vm((2, seqs), bf16), vm((seqs, width_in), f32), vm((seqs, rows), bf16),
         vm((EXPERTS, high, 128), bf16), vm((EXPERTS, high, 128), bf16),
         vm((4, rows, 128), f32), vm((rows, width_in), f32), vm((EXPERTS, high, 128), f32),
-        vm((rows, width_in), bf16),
-        vm((slots, width_in, width), bf16), vm((slots, width_in, width), bf16), vm((chunks, width, width_in), bf16),
+        vm((slots, 2, width_in, width), bf16), vm((chunks, width, width_in), bf16),
         vm((chunks, 2, rows, width), bf16), vm((chunks, 2, rows, half), bf16),
         vm((chunks, 2, rows, half), bf16), vm((chunks, 2, rows, half), f32),
         vm((chunks, 2, rows, quarter), bf16), vm((chunks, rows, width), bf16),
         vm((rows, width_in), f32), vm((EXPERTS, low, 128), f32),
         vm((blocks, EXPERTS, low, 128), bf16), vm((blocks, EXPERTS, low, 128), bf16),
-        dma((8,)), dma((slots,)), dma((slots,)), dma((chunks,)),
-    ] + [dma((3,))] * 4 + [dma((chunks,))] * 10 + [dma((blocks, 3))] * 2
+        dma((8,)), dma((slots,)), dma((chunks,)), dma((8,)), dma((1,)), dma((1,)),
+    ] + [dma((chunks,))] * 4 + [dma((blocks,))]
     anyspace = pl.BlockSpec(memory_space=pl.ANY)
     return pl.pallas_call(
         functools.partial(fused_kernel, dims),
-        out_shape=jax.ShapeDtypeStruct((seqs, width_in), bf16),
+        out_shape=pltpu.VMEM((seqs, width_in), bf16),
         in_specs=[anyspace] * 11,
         out_specs=pl.BlockSpec(memory_space=pltpu.VMEM),
         scratch_shapes=scratch,
         compiler_params=pltpu.CompilerParams(
-            collective_id=0, has_side_effects=True, vmem_limit_bytes=67043328
+            collective_id=0, has_side_effects=True, vmem_limit_bytes=66846720
         ),
     )(
         lengths.reshape(1, seqs), routes.T, tokens, jnp.transpose(queries, (1, 0, 2)), new_kv.reshape(2, nn, hd), cache_kv.reshape(2, nk, hd),

time: 37.5 us -> 34.3 us (0.915)
  Pallas kernels: 35.9 us -> 33.6 us
  local copies, waits for them, and re-layouts: 1.42 us -> 0.62 us
    pallas_call x1, Pallas kernels: 35.9 us -> 33.6 us  [fused(): pl.pallas_call(functools.partial(fused_kernel, dims), out_shape=pltpu.VME...]
    unnamed x1, local copies, waits for them, and re-layouts: 1.42 us -> 0.62 us
where the time goes in v2:
time: 34.3 us; the launch traced here: 34.2 us
  Pallas kernels  33.6 us (98%)
  local copies, waits for them, and re-layouts  0.62 us (2%)
    pallas_call x1, Pallas kernels, fused(): pl.pallas_call(functools.partial(fused_kernel, dims), out_shape=pltpu.VME...  33.6 us

profile of v2, /device:TPU:0, one launch (start us, length us, event | category | flops | bytes accessed | tf_op | source)
XLA Modules:
  0.0 34.2 jit_solution(17422821169597675502)
XLA Ops:
  0.0 33.6 %shard_map.109 = bf16[16,1536]{1,0:T(8,128)(2,1)S(1)} custom-call(s32[1,16]{1,0:T(1,128)} %bitcast.10, s32[2,16]{1,0:T(2,128)} %bitcast.9, bf16[16,1536]{1,0:T(8,128)(2,1)} %tokens_hbm.1, bf16[12,16,128]{2,1,0:T(8,128)(2,1)} %bitcast.7, bf16[2,32,128]{2,1,0:T(8,128)(2,1)} %bitcast.8, bf16[2,512,128]{2,1,0:T(8,128)(2,1)} %bitcast.6, f32[1536]{0:T(1024)} %gain_hbm.1, ...), custom_call_target="tpu_custom_call" | custom-call | tf_op jit(solution)/shard_map/pallas_call | solution.py:490
  33.6 0.6 %copy.13 = bf16[16,1536]{1,0:T(8,128)(2,1)} copy(bf16[16,1536]{1,0:T(8,128)(2,1)S(1)} %shard_map.109) | data formatting | bytes 98304

commit v3 on v2

--- a/solution.py
+++ b/solution.py
@@ -177,12 +177,12 @@
     def gate_copy(i):
         s = i % slots
         cols = pl.ds(i * width, width)
-        return pltpu.make_async_copy(gate_hbm.at[:, cols], lift_w.at[s, 0], lift_sem.at[s])
+        return pltpu.make_async_copy(gate_hbm.at[:, cols], lift_w.at[s, 0], lift_sem.at[s, 0])
 
     def up_copy(i):
         s = i % slots
         cols = pl.ds(i * width, width)
-        return pltpu.make_async_copy(up_hbm.at[:, cols], lift_w.at[s, 1], lift_sem.at[s])
+        return pltpu.make_async_copy(up_hbm.at[:, cols], lift_w.at[s, 1], lift_sem.at[s, 1])
 
     def down_copy(i):
         rws = pl.ds(i * width, width)
@@ -281,6 +281,11 @@
             device_id=(p, me, to), device_id_type=MESH,
         )
 
+    whole = rows - 8
+    upper = lax.broadcasted_iota(jnp.int32, (8, width), 0) < 4
+
+    last = chunks - 1
+
     def at_half(c):
         return pl.ds(pl.multiple_of(c * half, half), half)
 
@@ -291,10 +296,10 @@
     theirs = own * 2 + 1 - xpos
 
     def stage1(i):
-        return remote(part.at[i, :, :, at_half(1 - own)], got1.at[i], 2, s1_recv, i, sibling)
+        return remote(part.at[i, :, at_half(1 - own)], got1.at[i], 2, s1_recv, i, sibling)
 
     def stage2(i):
-        return remote(half16.at[i, :, :, at_quarter(1 - xpos)], got2.at[i], 3, s2_recv, i, partner)
+        return remote(half16.at[i, :, at_quarter(1 - xpos)], got2.at[i], 3, s2_recv, i, partner)
 
     def spread1(i):
         return remote(hid.at[i, :, at_quarter(mine)], hid.at[i, :, at_quarter(mine)], 4, h1_recv, i, partner)
@@ -312,13 +317,22 @@
             ss_copy(j).start()
 
     def direct(i):
-        return remote(hid.at[i, :, at_quarter(mine)], hid.at[i, :, at_quarter(mine)], 6, h2_recv, i, other)
+        return remote(
+            hid.at[i, :, at_quarter(mine)], hid.at[i, :, at_quarter(mine)], 6, h2_recv, chunks if i == last else i, other
+        )
 
     def multiply(i):
         s = i % slots
-        pltpu.make_async_copy(lift_w.at[s], lift_w.at[s], lift_sem.at[s]).wait()
-        part[i, 0] = jnp.dot(flat[...], lift_w[s, 0], preferred_element_type=f32).astype(bf16)
-        part[i, 1] = jnp.dot(flat[...], lift_w[s, 1], preferred_element_type=f32).astype(bf16)
+        gate_copy(i).wait()
+        if i < chunks - 2:
+            up_copy(i).wait()
+        g = jnp.dot(flat[...], lift_w[s, 0], preferred_element_type=f32)
+        part[i, :whole] = g[:whole].astype(bf16)
+        if i >= chunks - 2:
+            up_copy(i).wait()
+        u = jnp.dot(flat[...], lift_w[s, 1], preferred_element_type=f32)
+        part[i, whole : 2 * whole] = u[:whole].astype(bf16)
+        part[i, 2 * whole :] = jnp.where(upper, g[whole:], pltpu.roll(u[whole:], 4, 0)).astype(bf16)
         stage1(i).start()
         when(i == 0, exchange_squares)
 
@@ -331,10 +345,9 @@
 
     def add_core(b):
         stage1(b).wait_recv()
-        for n in range(2):
-            both = part[b, n, :, at_half(own)].astype(f32) + got1[b, n].astype(f32)
-            half32[b, n] = both
-            half16[b, n] = both.astype(bf16)
+        both = part[b, :, at_half(own)].astype(f32) + got1[b].astype(f32)
+        half32[b] = both
+        half16[b] = both.astype(bf16)
         stage2(b).start()
 
     def activate(c):
@@ -346,9 +359,13 @@
         when(c == 0, total)
         stage2(c).wait_recv()
         scale = lax.rsqrt(ss_rows[t][:, :1] / full_width + EPSILON)
-        g = (half32[c, 0, :, at_quarter(xpos)] + got2[c, 0].astype(f32)) * scale
-        u = (half32[c, 1, :, at_quarter(xpos)] + got2[c, 1].astype(f32)) * scale
-        hid[c, :, at_quarter(mine)] = (g / (1.0 + jnp.exp(-g)) * u).astype(bf16)
+        sums = half32[c, :, at_quarter(xpos)] + got2[c].astype(f32)
+        ends = sums[2 * whole :]
+        for place, g, u in (
+            (slice(0, whole), sums[:whole], sums[whole : 2 * whole]), (slice(whole, rows), ends, pltpu.roll(ends, 4, 0)),
+        ):
+            g, u = g * scale[place], u * scale[place]
+            hid[c, place, at_quarter(mine)] = (g / (1.0 + jnp.exp(-g)) * u).astype(bf16)
         spread1(c).start()
         spread2(c).start()
 
@@ -376,7 +393,6 @@
         when(i >= 4, lambda: activate(i - 4))
         when(i >= 7, lambda: hand_on(i - 7))
 
-    last = chunks - 1
     activate(last - 3)
     add_core(last)
     hand_on(last - 6)
@@ -390,7 +406,6 @@
     hand_on(last - 3)
     activate(last)
     project(last - 4)
-    hand_on(last - 2)
     project(last - 3)
     project(last - 2)
     project(last - 1)
@@ -403,10 +418,18 @@
         )
 
     wide = acc.shape[1] // blocks
-    ready(last)
+
+    def share(n, cols):
+        return jnp.dot(hid[last, :, at_quarter(n)], down_w[last, at_quarter(n), cols], preferred_element_type=f32)
+
+    down_copy(last).wait()
+    spread2(last).wait_recv()
+    acc[...] += share(xpos, slice(None)) + share(2 + xpos, slice(None))
+    spread1(last).wait_recv()
+    direct(last).wait_recv()
     for b in range(blocks):
         cols = slice(b * wide, (b + 1) * wide)
-        acc[:, cols] += jnp.dot(hid[last], down_w[last, :, cols], preferred_element_type=f32)
+        acc[:, cols] += share(1 - xpos, cols) + share(3 - xpos, cols)
         fold(acc.at[:, cols], rtall, ret_send.at[b])
         for j in (2, 3, 1):
             give(b, j).start()
@@ -449,7 +472,7 @@
             flat[e * CAP : (e + 1) * CAP, j * 128 : (j + 1) * 128] = tall[e, j * CAP : (j + 1) * CAP]
 
 
-DIRECT = 2
+DIRECT = 3
 
 
 def fused(
@@ -463,6 +486,7 @@
     chunks = ff // width
     slots = min(5, chunks)
     rows = -(-EXPERTS * CAP // 8) * 8
+    dense = 2 * rows - 8
     full_width = width_in * lax.axis_size("tensor")
     blocks = 2
     dims = (seqs, heads, heads // kvh, hd, ctx, kvh, full_width, chunks, width, slots, rows, blocks)
@@ -479,13 +503,13 @@
         vm((EXPERTS, high, 128), bf16), vm((EXPERTS, high, 128), bf16),
         vm((4, rows, 128), f32), vm((rows, width_in), f32), vm((EXPERTS, high, 128), f32),
         vm((slots, 2, width_in, width), bf16), vm((chunks, width, width_in), bf16),
-        vm((chunks, 2, rows, width), bf16), vm((chunks, 2, rows, half), bf16),
-        vm((chunks, 2, rows, half), bf16), vm((chunks, 2, rows, half), f32),
-        vm((chunks, 2, rows, quarter), bf16), vm((chunks, rows, width), bf16),
+        vm((chunks, dense, width), bf16), vm((chunks, dense, half), bf16),
+        vm((chunks, dense, half), bf16), vm((chunks, dense, half), f32),
+        vm((chunks, dense, quarter), bf16), vm((chunks, rows, width), bf16),
         vm((rows, width_in), f32), vm((EXPERTS, low, 128), f32),
         vm((blocks, EXPERTS, low, 128), bf16), vm((blocks, EXPERTS, low, 128), bf16),
-        dma((8,)), dma((slots,)), dma((chunks,)), dma((8,)), dma((1,)), dma((1,)),
-    ] + [dma((chunks,))] * 4 + [dma((blocks,))]
+        dma((8,)), dma((slots, 2)), dma((chunks,)), dma((8,)), dma((1,)), dma((1,)),
+    ] + [dma((chunks,))] * 3 + [dma((chunks + 1,)), dma((blocks,))]
     anyspace = pl.BlockSpec(memory_space=pl.ANY)
     return pl.pallas_call(
         functools.partial(fused_kernel, dims),

time: 34.3 us -> 33.8 us (0.985)
  Pallas kernels: 33.6 us -> 33 us
    pallas_call x1, Pallas kernels: 33.6 us -> 33 us  [fused(): pl.pallas_call(functools.partial(fused_kernel, dims), out_shape=pltpu.VME...]
where the time goes in v3:
time: 33.8 us; the launch traced here: 33.7 us
  Pallas kernels  33 us (98%)
  local copies, waits for them, and re-layouts  0.62 us (2%)
    pallas_call x1, Pallas kernels, fused(): pl.pallas_call(functools.partial(fused_kernel, dims), out_shape=pltpu.VME...  33 us

profile of v3, /device:TPU:0, one launch (start us, length us, event | category | flops | bytes accessed | tf_op | source)
XLA Modules:
  0.0 33.7 jit_solution(16284438584156254195)
XLA Ops:
  0.0 33.0 %shard_map.109 = bf16[16,1536]{1,0:T(8,128)(2,1)S(1)} custom-call(s32[1,16]{1,0:T(1,128)} %bitcast.10, s32[2,16]{1,0:T(2,128)} %bitcast.9, bf16[16,1536]{1,0:T(8,128)(2,1)} %tokens_hbm.1, bf16[12,16,128]{2,1,0:T(8,128)(2,1)} %bitcast.7, bf16[2,32,128]{2,1,0:T(8,128)(2,1)} %bitcast.8, bf16[2,512,128]{2,1,0:T(8,128)(2,1)} %bitcast.6, f32[1536]{0:T(1024)} %gain_hbm.1, ...), custom_call_target="tpu_custom_call" | custom-call | tf_op jit(solution)/shard_map/pallas_call | solution.py:514
  33.0 0.6 %copy.13 = bf16[16,1536]{1,0:T(8,128)(2,1)} copy(bf16[16,1536]{1,0:T(8,128)(2,1)S(1)} %shard_map.109) | data formatting | bytes 98304

commit v4 on v3

--- a/solution.py
+++ b/solution.py
@@ -324,11 +324,11 @@
     def multiply(i):
         s = i % slots
         gate_copy(i).wait()
-        if i < chunks - 2:
+        if i < chunks - 3:
             up_copy(i).wait()
         g = jnp.dot(flat[...], lift_w[s, 0], preferred_element_type=f32)
         part[i, :whole] = g[:whole].astype(bf16)
-        if i >= chunks - 2:
+        if i >= chunks - 3:
             up_copy(i).wait()
         u = jnp.dot(flat[...], lift_w[s, 1], preferred_element_type=f32)
         part[i, whole : 2 * whole] = u[:whole].astype(bf16)

time: 33.8 us -> 33.8 us (level)
  no operation moved by 1% of the time
where the time goes in v4:
time: 33.8 us; the launch traced here: 33.7 us
  Pallas kernels  33 us (98%)
  local copies, waits for them, and re-layouts  0.62 us (2%)
    pallas_call x1, Pallas kernels, fused(): pl.pallas_call(functools.partial(fused_kernel, dims), out_shape=pltpu.VME...  33 us

profile of v4, /device:TPU:0, one launch (start us, length us, event | category | flops | bytes accessed | tf_op | source)
XLA Modules:
  0.0 33.7 jit_solution(17991645860806841967)
XLA Ops:
  0.0 33.0 %shard_map.109 = bf16[16,1536]{1,0:T(8,128)(2,1)S(1)} custom-call(s32[1,16]{1,0:T(1,128)} %bitcast.10, s32[2,16]{1,0:T(2,128)} %bitcast.9, bf16[16,1536]{1,0:T(8,128)(2,1)} %tokens_hbm.1, bf16[12,16,128]{2,1,0:T(8,128)(2,1)} %bitcast.7, bf16[2,32,128]{2,1,0:T(8,128)(2,1)} %bitcast.8, bf16[2,512,128]{2,1,0:T(8,128)(2,1)} %bitcast.6, f32[1536]{0:T(1024)} %gain_hbm.1, ...), custom_call_target="tpu_custom_call" | custom-call | tf_op jit(solution)/shard_map/pallas_call | solution.py:514
  33.0 0.6 %copy.13 = bf16[16,1536]{1,0:T(8,128)(2,1)} copy(bf16[16,1536]{1,0:T(8,128)(2,1)S(1)} %shard_map.109) | data formatting | bytes 98304
